TPU v7x, 32 devices: a whole 2x2x4 slice. The times are simulated.
32 devices in a mesh: dp: 16 (over z, y, x), tensor: 2 (over core).
Axes of the slice: x: 2, y: 2, z: 4, core: 2. Of those that a mesh axis runs over, the one named last changes fastest.
Arguments:
- residual: bfloat16 [512, 6144], P('dp', 'tensor'), may hold values from -16 to 16
- queries: bfloat16 [512, 6144], P('dp', 'tensor'), may hold values from -4.5 to 4.5
- keys: bfloat16 [512, 128, 1024], P('dp', None, 'tensor'), may hold values from -4.5 to 4.5
- values: bfloat16 [512, 128, 1024], P('dp', None, 'tensor'), may hold values from -6 to 6
- lengths: int32 [512], P('dp'), may hold values from 2 to 128
- norm_gain: bfloat16 [6144], P('tensor'), may hold values from 0.099609375 to 1.8984375
- expert_ids: int32 [512, 2], P('dp'), may hold values from 0 to 7, all different within a row; in each aligned block of 32 rows (0 to 31, 32 to 63, ...) at most 16 rows name the same one
- expert_weights: float32 [512, 2], P('dp'), may hold values from 0.2 to 1
- w_in: bfloat16 [6144, 65536], P('tensor', 'dp'), may hold values from -0.078125 to 0.078125
- w_out: bfloat16 [65536, 6144], P('dp', 'tensor'), may hold values from -0.0625 to 0.0625
Outputs:
- output: bfloat16 [512, 6144], P('dp', 'tensor')
Inputs may be any that keep to these rules, and one draw needn't show every extreme that they name: `expert_ids`: each token names 2 different experts; at most 16 of the tokens of one index of dp name one expert, and in every draw some expert is named by exactly 16 of them.
All inputs are finite; a program needn't handle non-finite values.
Results may differ from a plain program's by a relative error of at most 0.008.
Values may be sent and summed in bfloat16 or wider, within the bound.
A program may use at most 128 MiB of HBM per device.

v0:
```python
import jax
import jax.numpy as jnp
from jax import lax
from jax.sharding import PartitionSpec as P

D = 6144
HEADS = 48
KV = 8
HEAD = 128
EXPERTS = 8
TOPK = 2
CACHE = 128
SRC_CAP = 16
NORM_EPSILON = 1e-05


def prefix(part, axis, combine, identity):
    place = lax.axis_index(axis)
    gathered = lax.all_gather(part, axis)
    state = jnp.zeros_like(part) + jnp.asarray(identity, part.dtype)

    def one(lap, state):
        return combine(state, lax.dynamic_index_in_dim(gathered, lap, 0, False))

    return lax.fori_loop(0, place, one, state)


def add_counts(earlier, later):
    return earlier + later


def expert_rows(tok_rows, w_in, w_out):
    partial_sum = jnp.einsum("df,rd->fr", w_in, tok_rows, preferred_element_type=jnp.float32)
    hidden_total = lax.psum(partial_sum.astype(jnp.bfloat16), "tensor").astype(jnp.float32)
    hidden = jax.nn.silu(hidden_total).astype(jnp.bfloat16)
    return jnp.einsum("fr,fd->rd", hidden, w_out, preferred_element_type=jnp.float32)


def shards(
    residual, queries, keys, values, lengths, norm_gain, expert_ids, expert_weights, w_in, w_out
):
    tokens = residual.shape[0]
    width_local = residual.shape[1]
    head_groups = keys.shape[2] // HEAD
    group_size = HEADS // KV
    query_rows = queries.reshape(tokens, head_groups, group_size, HEAD)
    key_rows = keys.reshape(tokens, CACHE, head_groups, HEAD)
    value_rows = values.reshape(tokens, CACHE, head_groups, HEAD)
    scores = jnp.einsum(
        "tgjd,tlgd->tgjl", query_rows, key_rows, preferred_element_type=jnp.float32
    ) * HEAD ** (-0.5)
    live_mask = (jnp.arange(CACHE, dtype=jnp.int32)[None, :] < lengths[:, None])[:, None, None, :]
    scores = jnp.where(live_mask, scores, -1e30)
    peak_score = jnp.max(scores, axis=-1, keepdims=True)
    powered = jnp.exp(scores - peak_score)
    attention_probs = (powered / jnp.sum(powered, axis=-1, keepdims=True)).astype(jnp.bfloat16)
    attended = jnp.einsum(
        "tgjl,tlgd->tgjd", attention_probs, value_rows, preferred_element_type=jnp.float32
    )
    summed = residual.astype(jnp.float32) + attended.reshape(tokens, width_local)
    square_sums = lax.psum(jnp.sum(summed * summed, axis=1), "tensor")
    normed = (
        summed
        * lax.rsqrt(square_sums[:, None] / D + NORM_EPSILON)
        * norm_gain.astype(jnp.float32)[None, :]
    ).astype(jnp.bfloat16)
    flat_ids = expert_ids.reshape(-1)
    expert_iota = jnp.arange(EXPERTS, dtype=jnp.int32)
    onehot = (flat_ids[:, None] == expert_iota[None, :]).astype(jnp.int32)
    local_rank = jnp.sum(
        (jnp.cumsum(onehot, axis=0, dtype=jnp.int32) - onehot) * onehot, axis=1, dtype=jnp.int32
    )
    counts = jnp.sum(onehot, axis=0, dtype=jnp.int32)
    offsets = prefix(counts, "dp", add_counts, jnp.zeros_like(counts))
    slot_index = local_rank + jnp.sum(onehot * offsets[None, :], axis=1, dtype=jnp.int32)
    capacity = tokens * lax.axis_size("dp") * TOPK * 3 // (4 * EXPERTS)
    keep_mask = slot_index < capacity
    owners = lax.axis_size("dp") // EXPERTS
    slot_total = EXPERTS * SRC_CAP
    pair_target = flat_ids * SRC_CAP + local_rank
    pick_pairs = pair_target[None, :] == jnp.arange(slot_total, dtype=jnp.int32)[:, None]
    pick_tokens = jnp.sum(
        pick_pairs.reshape(slot_total, tokens, TOPK).astype(jnp.float32), axis=2
    ).astype(jnp.bfloat16)
    packed = jnp.dot(pick_tokens, normed, preferred_element_type=jnp.float32).astype(jnp.bfloat16)
    outgoing = jnp.broadcast_to(
        packed.reshape(EXPERTS, 1, SRC_CAP, width_local), (EXPERTS, owners, SRC_CAP, width_local)
    )
    outgoing = outgoing.reshape(EXPERTS * owners, SRC_CAP, width_local)
    received = lax.all_to_all(outgoing, "dp", split_axis=0, concat_axis=0, tiled=True)
    total_rows = received.shape[0] * received.shape[1]
    results = expert_rows(received.reshape(total_rows, width_local), w_in, w_out)
    returned = results.reshape(received.shape[0], SRC_CAP, width_local)
    combined = lax.all_to_all(
        returned.astype(jnp.bfloat16), "dp", split_axis=0, concat_axis=0, tiled=True
    ).astype(returned.dtype)
    per_expert = jnp.sum(combined.reshape(EXPERTS, owners, SRC_CAP, width_local), axis=1).reshape(
        slot_total, width_local
    )
    pair_weight = expert_weights.reshape(-1) * keep_mask.astype(jnp.float32)
    mix_rows = jnp.sum(
        (pick_pairs.astype(jnp.float32) * pair_weight[None, :]).reshape(slot_total, tokens, TOPK),
        axis=2,
    )
    addition = jnp.einsum("st,sd->td", mix_rows, per_expert, precision=lax.Precision.HIGHEST)
    return (summed + addition).astype(jnp.bfloat16)


def solution(mesh):
    in_specs = (
        P("dp", "tensor"),
        P("dp", "tensor"),
        P("dp", None, "tensor"),
        P("dp", None, "tensor"),
        P("dp"),
        P("tensor"),
        P("dp", None),
        P("dp", None),
        P("tensor", "dp"),
        P("dp", "tensor"),
    )
    out_specs = P("dp", "tensor")
    return jax.shard_map(shards, mesh=mesh, in_specs=in_specs, out_specs=out_specs, check_vma=False)
```

profile of v0, /device:TPU:0, one launch (start us, length us, event | category | flops | bytes accessed | tf_op | source)
XLA Modules:
  0.0 180.8 jit_solution(6086627197087808506)
XLA Ops:
  6.5 0.8 copy.37
  7.3 0.1 eq.30
  7.6 0.7 iota_compare_fusion.2
  8.3 0.7 convert_element_type.53
  9.0 1.2 dynamic-slice
  10.8 0.2 dynamic-update-slice
  11.1 16.2 %all-reduce = s32[128]{0:T(128)S(1)} all-reduce(s32[128]{0:T(128)S(1)} %dynamic-update-slice), channel_id=2, replica_groups=mesh['dp'=16,'tensor'=2] {'dp'}, use_global_device_ids=true, to_apply=%add | all-reduce | flops 128 | bytes 1024
  27.5 0.2 select_reduce_fusion.1
  27.8 0.1 reduce_sum.78
  28.0 0.7 multiply_add_fusion
  28.7 1.2 reshape.102
  29.9 4.6 %fusion.30 = (f32[32,4,6]{2,1,0:T(4,128)S(1)}, f32[32,4,6,128]{3,2,1,0:T(8,128)S(1)}) fusion(bf16[32,4,6,128]{3,2,1,0:T(8,128)(2,1)S(1)} %reshape.102, pred[32,128]{1,0:T(8,128)(4,1)S(1)} %iota_compare_fusion.2, bf16[32,128,512]{2,1,0:T(8,128)(2,1)} %param.14), kind=kOutput, calls=%fused_computation.47 | convolution fusion | flops 25559168 | bytes 4791296 | tf_op jit(solution)/shard_map/sub | solution.py:55
  34.6 3.5 %fusion.6 = f32[32,4,6,128]{3,2,1,0:T(8,128)S(1)} fusion(f32[32,4,6,128]{3,2,1,0:T(8,128)S(1)} %get-tuple-element.42, f32[32,4,6]{2,1,0:T(4,128)S(1)} %get-tuple-element.41, bf16[32,128,512]{2,1,0:T(8,128)(2,1)} %param.15), kind=kOutput, calls=%fused_computation.10 | convolution fusion | flops 25362432 | bytes 4983808 | tf_op jit(solution)/shard_map/tgjl,tlgd->tgjd/dot_general | solution.py:57
  38.2 0.2 multiply_reduce_fusion
  38.3 2.5 %psum.14 = f32[32]{0:T(128)S(1)} all-reduce(f32[32]{0:T(128)S(1)} %multiply_reduce_fusion), channel_id=1, replica_groups=mesh['dp'=16,'tensor'=2] {'tensor'}, use_global_device_ids=true, to_apply=%region_11.12 | all-reduce | flops 32 | bytes 256 | tf_op jit(solution)/shard_map/psum | solution.py:61
  40.9 0.4 convolution_convert_fusion.2
  41.3 0.2 broadcast_in_dim.19
  41.5 40.8 %all_to_all.10 = bf16[16,16,3072]{2,1,0:T(8,128)(2,1)S(1)} all-to-all(bf16[16,16,3072]{2,1,0:T(8,128)(2,1)S(1)} %bitcast.44), channel_id=1, replica_groups=mesh['dp'=16,'tensor'=2] {'dp'}, dimensions={0} | all-to-all | bytes 3145728 | tf_op jit(solution)/shard_map/all_to_all | solution.py:90
  82.3 13.2 %fusion.1 = bf16[4096,256]{0,1:T(8,128)(2,1)} fusion(bf16[256,3072]{1,0:T(8,128)(2,1)S(1)} %bitcast.46, bf16[3072,4096]{1,0:T(8,128)(2,1)} %param.20), kind=kOutput, calls=%fused_computation.5 | convolution fusion | flops 6443499520 | bytes 28835840 | tf_op jit(solution)/shard_map/df,rd->fr/dot_general | solution.py:33
  95.5 19.7 %all-reduce.3.cloned.1.call-done = bf16[4096,256]{0,1:T(8,128)(2,1)} async-done(((bf16[4096,256]{0,1:T(8,128)(2,1)}), bf16[4096,256]{0,1:T(8,128)(2,1)}) %all-reduce.3.cloned.1.call-update) | async-done | bytes 2097168 | tf_op jit(solution)/shard_map/psum | solution.py:34
  115.3 12.2 %convolution_convert_fusion.1 = bf16[256,3072]{1,0:T(8,128)(2,1)S(1)} fusion(bf16[4096,3072]{1,0:T(8,128)(2,1)} %param.21, bf16[4096,256]{0,1:T(8,128)(2,1)} %all-reduce.3.cloned.1.call-done), kind=kOutput, calls=%fused_computation.16 | convolution fusion | flops 6449528832 | bytes 28835840 | tf_op jit(solution)/shard_map/fr,fd->rd/dot_general | solution.py:36
  127.5 44.6 %all_to_all.11 = bf16[16,16,3072]{2,1,0:T(8,128)(2,1)S(1)} all-to-all(bf16[16,16,3072]{2,1,0:T(8,128)(2,1)S(1)} %bitcast.47), channel_id=1, replica_groups=mesh['dp'=16,'tensor'=2] {'dp'}, dimensions={0} | all-to-all | bytes 3145728 | tf_op jit(solution)/shard_map/all_to_all | solution.py:94
  172.0 0.3 convert_reduce_fusion
  172.4 1.6 fusion.12
  (20 shorter events, 0.8 us)
Async XLA Ops:
  6.5 108.7 %all-reduce.3.cloned.1.call-start = ((), (), s32[]{:S(2)}) async-start(), calls=%async_computation.2 | async-start | bytes 4194304 | tf_op jit(solution)/shard_map/psum | solution.py:34
  34.5 3.6 %copy-start = (bf16[32,3072]{1,0:T(8,128)(2,1)S(1)}, bf16[32,3072]{1,0:T(8,128)(2,1)}, u32[]{:S(2)}) copy-start(bf16[32,3072]{1,0:T(8,128)(2,1)} %param.12) | copy-start | bytes 589828
  34.6 6.2 %copy-start.1 = (f32[32,2]{0,1:T(2,128)S(1)}, f32[32,2]{0,1:T(2,128)}, u32[]{:S(2)}) copy-start(f32[32,2]{0,1:T(2,128)} %param.19) | copy-start | bytes 772
Sparse Core Ops, SparseCore 0:
  95.6 19.5 all-reduce.2
where the time goes:
time: 181 us
  blocking collectives  104 us (57%)
  matrix products  35.5 us (20%)
  waiting for transfers between devices  19.8 us (11%)
  between operations  14.1 us (8%)
  local copies, waits for them, and re-layouts  4.26 us (2%)
  other arithmetic  3.15 us (2%)
    all_to_all x1, blocking collectives, shards(): lax.all_to_all(returned.astype(jnp.bfloat16), 'dp', split_axis=0, concat_...  44.6 us
    all_to_all x1, blocking collectives, shards(): lax.all_to_all(outgoing, 'dp', split_axis=0, concat_axis=0, tiled=True)  40.8 us
    psum x1, waiting for transfers between devices, expert_rows(): lax.psum(partial_sum.astype(jnp.bfloat16), 'tensor').astype(jnp.float32)  19.7 us
    unnamed x1, blocking collectives  16.2 us
    dot_general x1, matrix products, expert_rows(): jnp.einsum('df,rd->fr', w_in, tok_rows, preferred_element_type=jnp.float32)  13.2 us
    dot_general x1, matrix products, expert_rows(): jnp.einsum('fr,fd->rd', hidden, w_out, preferred_element_type=jnp.float32)  12.2 us
    sub x1, matrix products, shards(): powered = jnp.exp(scores - peak_score)  4.65 us
  transfers between devices with their start and end apart: 1, of which 1 were waited for; matrix products, arithmetic and copies ran while one was open for 0% of the time, Pallas kernels for 0%

commit v1 on v0

--- a/solution.py
+++ b/solution.py
@@ -30,8 +30,12 @@
 
 
 def expert_rows(tok_rows, w_in, w_out):
+
+    def replace_types_in(xx):
+        return lax.all_gather(xx, "tensor").sum(axis=0)
+
     partial_sum = jnp.einsum("df,rd->fr", w_in, tok_rows, preferred_element_type=jnp.float32)
-    hidden_total = lax.psum(partial_sum.astype(jnp.bfloat16), "tensor").astype(jnp.float32)
+    hidden_total = replace_types_in(partial_sum.astype(jnp.bfloat16)).astype(jnp.float32)
     hidden = jax.nn.silu(hidden_total).astype(jnp.bfloat16)
     return jnp.einsum("fr,fd->rd", hidden, w_out, preferred_element_type=jnp.float32)
 

time: 181 us -> 193 us (1.066)
  other arithmetic: 3.15 us -> 14.9 us
  local copies, waits for them, and re-layouts: 4.26 us -> 12.1 us
  waiting for transfers between devices: 19.8 us -> 12.1 us
    psum x1 -> x0, waiting for transfers between devices: 19.7 us -> none  [expert_rows(): lax.psum(partial_sum.astype(jnp.bfloat16), 'tensor').astype(jnp.float32)]
    all_gather x0 -> x1, waiting for transfers between devices: none -> 12.1 us  [replace_types_in(): return lax.all_gather(xx, 'tensor').sum(axis=0)]
    reduce_sum x0 -> x1, other arithmetic: none -> 11.7 us  [replace_types_in(): return lax.all_gather(xx, 'tensor').sum(axis=0)]
    all_gather x0 -> x1, local copies, waits for them, and re-layouts: none -> 7.8 us  [replace_types_in(): return lax.all_gather(xx, 'tensor').sum(axis=0)]
where the time goes in v1:
time: 193 us; the launch traced here: 192 us
  blocking collectives  104 us (54%)
  matrix products  35.3 us (18%)
  other arithmetic  14.9 us (8%)
  between operations  14.1 us (7%)
  local copies, waits for them, and re-layouts  12.1 us (6%)
  waiting for transfers between devices  12.1 us (6%)
    all_to_all x1, blocking collectives, shards(): lax.all_to_all(returned.astype(jnp.bfloat16), 'dp', split_axis=0, concat_...  44.5 us
    all_to_all x1, blocking collectives, shards(): lax.all_to_all(outgoing, 'dp', split_axis=0, concat_axis=0, tiled=True)  40.8 us
    unnamed x1, blocking collectives  16.2 us
    dot_general x1, matrix products, expert_rows(): jnp.einsum('df,rd->fr', w_in, tok_rows, preferred_element_type=jnp.float32)  13.2 us
    all_gather x1, waiting for transfers between devices, replace_types_in(): return lax.all_gather(xx, 'tensor').sum(axis=0)  12.1 us
    dot_general x1, matrix products, expert_rows(): jnp.einsum('fr,fd->rd', hidden, w_out, preferred_element_type=jnp.float32)  11.9 us
    reduce_sum x1, other arithmetic, replace_types_in(): return lax.all_gather(xx, 'tensor').sum(axis=0)  11.7 us
    all_gather x1, local copies, waits for them, and re-layouts, replace_types_in(): return lax.all_gather(xx, 'tensor').sum(axis=0)  7.8 us
  transfers between devices with their start and end apart: 1, of which 1 were waited for; matrix products, arithmetic and copies ran while one was open for 0% of the time, Pallas kernels for 0%

profile of v1, /device:TPU:0, one launch (start us, length us, event | category | flops | bytes accessed | tf_op | source)
XLA Modules:
  0.0 192.4 jit_solution(11840857165363939411)
XLA Ops:
  6.5 0.8 copy.45
  7.6 0.7 iota_compare_fusion.2
  8.3 0.7 convert_element_type.55
  9.0 1.2 dynamic-slice
  10.8 0.2 dynamic-update-slice
  11.1 16.2 %all-reduce = s32[128]{0:T(128)S(1)} all-reduce(s32[128]{0:T(128)S(1)} %dynamic-update-slice), channel_id=2, replica_groups=mesh['dp'=16,'tensor'=2] {'dp'}, use_global_device_ids=true, to_apply=%add | all-reduce | flops 128 | bytes 1024
  27.5 0.2 select_reduce_fusion.1
  28.0 0.7 multiply_add_fusion
  28.7 1.2 reshape.102
  29.9 4.6 %fusion.30 = (f32[32,4,6]{2,1,0:T(4,128)S(1)}, f32[32,4,6,128]{3,2,1,0:T(8,128)S(1)}) fusion(bf16[32,4,6,128]{3,2,1,0:T(8,128)(2,1)S(1)} %reshape.102, pred[32,128]{1,0:T(8,128)(4,1)S(1)} %iota_compare_fusion.2, bf16[32,128,512]{2,1,0:T(8,128)(2,1)} %param.14), kind=kOutput, calls=%fused_computation.47 | convolution fusion | flops 25559168 | bytes 4791296 | tf_op jit(solution)/shard_map/sub | solution.py:59
  34.6 3.5 %fusion.6 = f32[32,4,6,128]{3,2,1,0:T(8,128)S(1)} fusion(f32[32,4,6,128]{3,2,1,0:T(8,128)S(1)} %get-tuple-element.42, f32[32,4,6]{2,1,0:T(4,128)S(1)} %get-tuple-element.41, bf16[32,128,512]{2,1,0:T(8,128)(2,1)} %param.15), kind=kOutput, calls=%fused_computation.10 | convolution fusion | flops 25362432 | bytes 4983808 | tf_op jit(solution)/shard_map/tgjl,tlgd->tgjd/dot_general | solution.py:61
  38.2 0.2 multiply_reduce_fusion
  38.3 2.5 %psum.7 = f32[32]{0:T(128)S(1)} all-reduce(f32[32]{0:T(128)S(1)} %multiply_reduce_fusion), channel_id=1, replica_groups=mesh['dp'=16,'tensor'=2] {'tensor'}, use_global_device_ids=true, to_apply=%region_11.12 | all-reduce | flops 32 | bytes 256 | tf_op jit(solution)/shard_map/psum | solution.py:65
  40.9 0.4 convolution_convert_fusion.2
  41.3 0.2 broadcast_in_dim.19
  41.5 40.8 %all_to_all.10 = bf16[16,16,3072]{2,1,0:T(8,128)(2,1)S(1)} all-to-all(bf16[16,16,3072]{2,1,0:T(8,128)(2,1)S(1)} %bitcast.46), channel_id=1, replica_groups=mesh['dp'=16,'tensor'=2] {'dp'}, dimensions={0} | all-to-all | bytes 3145728 | tf_op jit(solution)/shard_map/all_to_all | solution.py:94
  82.3 13.2 %fusion.1 = bf16[4096,256]{0,1:T(8,128)(2,1)} fusion(bf16[256,3072]{1,0:T(8,128)(2,1)S(1)} %bitcast.48, bf16[3072,4096]{1,0:T(8,128)(2,1)} %param.20), kind=kOutput, calls=%fused_computation.5 | convolution fusion | flops 6443499520 | bytes 28835840 | tf_op jit(solution)/shard_map/df,rd->fr/dot_general | solution.py:37
  95.6 12.1 %all-gather.4.cloned.1.call-done = bf16[8192,256]{0,1:T(8,128)(2,1)} async-done(((bf16[4096,256]{0,1:T(8,128)(2,1)}), bf16[8192,256]{0,1:T(8,128)(2,1)}) %all-gather.4.cloned.1.call-update) | async-done | bytes 4194320 | tf_op jit(solution)/shard_map/all_gather | solution.py:35
  107.6 7.8 %reshape.114 = bf16[2,4096,256]{1,0,2:T(2,128)(2,1)} reshape(bf16[8192,256]{0,1:T(8,128)(2,1)} %all-gather.4.cloned.1.call-done) | data formatting | bytes 8388608 | tf_op jit(solution)/shard_map/all_gather | solution.py:35
  115.5 11.7 %reduce_sum.97 = bf16[4096,256]{0,1:T(8,128)(2,1)S(1)} reduce(bf16[2,4096,256]{1,0,2:T(2,128)(2,1)} %reshape.114, bf16[]{:T(256)} %constant.44.clone.1), dimensions={0}, to_apply=%region_12.13 | reduce | flops 1048576 | bytes 6291458 | tf_op jit(solution)/shard_map/reduce_sum | solution.py:35
  127.2 11.9 %convolution_convert_fusion.1 = bf16[256,3072]{1,0:T(8,128)(2,1)S(1)} fusion(bf16[4096,3072]{1,0:T(8,128)(2,1)} %param.21, bf16[4096,256]{0,1:T(8,128)(2,1)S(1)} %reduce_sum.97), kind=kOutput, calls=%fused_computation.16 | convolution fusion | flops 6449528832 | bytes 28835840 | tf_op jit(solution)/shard_map/fr,fd->rd/dot_general | solution.py:40
  139.1 44.5 %all_to_all.11 = bf16[16,16,3072]{2,1,0:T(8,128)(2,1)S(1)} all-to-all(bf16[16,16,3072]{2,1,0:T(8,128)(2,1)S(1)} %bitcast.49), channel_id=1, replica_groups=mesh['dp'=16,'tensor'=2] {'dp'}, dimensions={0} | all-to-all | bytes 3145728 | tf_op jit(solution)/shard_map/all_to_all | solution.py:98
  183.6 0.3 convert_reduce_fusion
  184.0 1.6 fusion.12
  (22 shorter events, 1.1 us)
Async XLA Ops:
  6.5 101.1 %all-gather.4.cloned.1.call-start = ((), (), s32[]{:S(2)}) async-start(), calls=%async_computation.2 | async-start | bytes 6291456 | tf_op jit(solution)/shard_map/all_gather | solution.py:35
  34.5 3.6 %copy-start = (bf16[32,3072]{1,0:T(8,128)(2,1)S(1)}, bf16[32,3072]{1,0:T(8,128)(2,1)}, u32[]{:S(2)}) copy-start(bf16[32,3072]{1,0:T(8,128)(2,1)} %param.12) | copy-start | bytes 589828
  34.6 6.2 %copy-start.1 = (f32[32,2]{0,1:T(2,128)S(1)}, f32[32,2]{0,1:T(2,128)}, u32[]{:S(2)}) copy-start(f32[32,2]{0,1:T(2,128)} %param.19) | copy-start | bytes 772
Sparse Core Ops, SparseCore 0:
  95.7 11.9 all-gather.3
